TPU v7x, 32 devices: a whole 2x2x4 slice. The times are simulated.
32 devices in a mesh: dp: 16 (over z, y, core), tensor: 2 (over x).
Axes of the slice: x: 2, y: 2, z: 4, core: 2. Of those that a mesh axis runs over, the one named last changes fastest.
Arguments:
- step: int32 [1], replicated, may hold values from 0 to 999
- activations: bfloat16 [2, 16384, 8192], P(None, 'dp', 'tensor'), may hold values from -6 to 6
- grad_weight: bfloat16 [2, 8192, 28672], P(None, 'tensor', 'dp'), may hold values from -6 to 6
Outputs:
- preconditioned: float32 [8192, 28672], P('tensor', 'dp')
All inputs are finite; a program needn't handle non-finite values.
Results may differ from a plain program's by a relative error of at most 0.0044.
Values may be sent and summed in bfloat16 or wider, within the bound.
No kernel may reach another device: no remote copies, remote signals or barrier semaphores. Data moves between devices by JAX's collectives and lax.ppermute only.
A program may use at most 192 MiB of HBM per device.

v0:
```python
import jax
import jax.numpy as jnp
from jax import lax
from jax.sharding import PartitionSpec as P

BLOCK = 1024
LAYERS = 2
ITERS = 4


def local(step, activations, grad_weight):
    groups = lax.axis_size("dp")
    layer = step[0] % LAYERS
    damping = 0.05 + 0.1 * step[0].astype(jnp.float32) / 1000.0
    acts = lax.dynamic_index_in_dim(activations, layer, 0, keepdims=False)
    grads = lax.dynamic_index_in_dim(grad_weight, layer, 0, keepdims=False)
    tok_rows = acts.shape[0]
    width = acts.shape[1]
    nblock = width // BLOCK
    share = BLOCK // groups
    blocks = acts.reshape(tok_rows, nblock, BLOCK)
    total_tokens = tok_rows * groups
    first = lax.axis_index("dp") * share
    summed = lax.psum(
        jnp.einsum("tkr,tkc->rkc", blocks, blocks, preferred_element_type=jnp.float32), "dp"
    )
    gram_rows = lax.dynamic_slice_in_dim(summed, first, share, 0)
    row_ids = first + lax.broadcasted_iota(jnp.int32, (share, 1, BLOCK), 0)
    col_ids = lax.broadcasted_iota(jnp.int32, (share, 1, BLOCK), 2)
    identity = (row_ids == col_ids).astype(jnp.float32)
    factor = gram_rows / total_tokens + damping * identity
    block_squares = lax.psum(jnp.sum(factor * factor, axis=(0, 2)), "dp")
    largest = lax.pmax(jnp.max(block_squares), "tensor")
    iterate = jnp.broadcast_to(identity / jnp.sqrt(largest), factor.shape)
    for sweep in range(ITERS):
        whole = lax.all_gather(iterate, "dp", axis=0, tiled=True)
        product = jnp.einsum("rkj,jkc->rkc", factor, whole, precision=lax.Precision.HIGHEST)
        iterate = 2.0 * iterate - jnp.einsum(
            "rkj,jkc->rkc", product, whole, precision=lax.Precision.HIGHEST
        )
    inverse = iterate.astype(jnp.bfloat16)
    stacked = grads.reshape(nblock, BLOCK, grads.shape[1])
    result = jnp.einsum(
        "rkc,kcf->krf",
        lax.all_gather(inverse, "dp", axis=0, tiled=True),
        stacked,
        preferred_element_type=jnp.float32,
    )
    return result.reshape(width, grads.shape[1])


def solution(mesh):
    in_specs = (P(), P(None, "dp", "tensor"), P(None, "tensor", "dp"))
    out_specs = P("tensor", "dp")
    return jax.shard_map(local, mesh=mesh, in_specs=in_specs, out_specs=out_specs, check_vma=False)
```

profile of v0, /device:TPU:0, one launch (start us, length us, event | category | flops | bytes accessed | tf_op | source)
XLA Modules:
  0.0 1019.5 jit_solution(3891566731821359104)
XLA Ops:
  7.2 7.9 constant_dynamic-slice_fusion.1
  15.1 12.0 %copy.23 = bf16[1,1024,4096]{1,2,0:T(8,128)(2,1)} copy(bf16[1,1024,4096]{2,1,0:T(8,128)(2,1)} %constant_dynamic-slice_fusion.1) | data formatting | bytes 16777216
  27.1 17.1 %convolution_bitcast_fusion = f32[1024,4,1024]{2,0,1:T(8,128)} fusion(bf16[1024,4,1024]{0,2,1:T(8,128)(2,1)} %bitcast.51), kind=kOutput, calls=%fused_computation | convolution fusion | flops 8589934592 | bytes 25165824 | tf_op jit(solution)/shard_map/tkr,tkc->rkc/dot_general | solution.py:25
  44.2 0.0 all-reduce.2.cloned.1.call-update
  44.3 0.0 all-gather.14.cloned.1.call-start
  44.3 0.1 fusion.18
  44.4 300.7 %all-reduce.2.cloned.1.call-done = f32[1024,4,1024]{2,0,1:T(8,128)} async-done(((f32[1024,4,1024]{2,0,1:T(8,128)}), f32[1024,4,1024]{2,0,1:T(8,128)}) %all-reduce.2.cloned.1.call-update) | async-done | bytes 16777232 | tf_op jit(solution)/shard_map/psum | solution.py:24
  345.1 1.5 multiply_reduce_fusion
  346.6 31.8 %psum.15 = f32[4]{0:T(128)S(1)} all-reduce(f32[4]{0:T(128)S(1)} %multiply_reduce_fusion), channel_id=1, replica_groups=mesh['dp'=16,'tensor'=2] {'dp'}, use_global_device_ids=true, to_apply=%region_2.3 | all-reduce | flops 4 | bytes 32 | tf_op jit(solution)/shard_map/psum | solution.py:32
  378.4 0.6 reduce_max.9
  379.0 5.5 pmax.7
  385.2 0.8 broadcast_multiply_fusion
  386.0 0.0 all-gather.14.cloned.1.call-update
  386.0 0.3 all-gather.6.cloned.1.call-start
  386.3 47.5 %all-gather.14.cloned.1.call-done = f32[1024,1024]{1,0:T(8,128)} async-done(((f32[64,1024]{1,0:T(8,128)}), f32[1024,1024]{1,0:T(8,128)}) %all-gather.14.cloned.1.call-update) | async-done | bytes 4194320 | tf_op jit(solution)/shard_map/all_gather | solution.py:36
  433.8 11.8 %fusion.4 = f32[64,4,1024]{2,0,1:T(8,128)S(1)} fusion(f32[1024,1024]{1,0:T(8,128)} %all-gather.14.cloned.1.call-done, f32[1024,4,1024]{2,0,1:T(8,128)} %all-reduce.2.cloned.1.call-done, s32[]{:T(128)S(6)} %select_n.18, f32[64,1024]{1,0:T(8,128)S(1)} %fusion.18), kind=kOutput, calls=%fused_computation.5 | convolution fusion | flops 3221749760 | bytes 6553604 | tf_op jit(solution)/shard_map/rkj,jkc->rkc/dot_general | solution.py:37
  445.6 12.8 %fusion.10 = f32[64,4,1024]{2,0,1:T(8,128)} fusion(f32[64,4,1024]{2,0,1:T(8,128)S(1)} %fusion.4, f32[1024,1024]{1,0:T(8,128)} %all-gather.14.cloned.1.call-done, f32[64,1024]{1,0:T(8,128)S(1)} %get-tuple-element.5), kind=kOutput, calls=%fused_computation.7 | convolution fusion | flops 3221487616 | bytes 6553600 | tf_op jit(solution)/shard_map/rkj,jkc->rkc/dot_general | solution.py:38
  458.4 0.0 all-gather.8.cloned.1.call-start
  458.4 125.1 %all-gather.6.cloned.1.call-done = f32[1024,4,1024]{2,0,1:T(8,128)} async-done(((f32[64,4,1024]{2,0,1:T(8,128)}), f32[1024,4,1024]{2,0,1:T(8,128)}) %all-gather.6.cloned.1.call-update) | async-done | bytes 16777232 | tf_op jit(solution)/shard_map/all_gather | solution.py:36
  583.5 15.3 %convolution_bitcast_fusion.6 = f32[64,4,1024]{2,0,1:T(8,128)S(1)} fusion(f32[1024,4,1024]{2,0,1:T(8,128)} %all-gather.6.cloned.1.call-done, f32[1024,4,1024]{2,0,1:T(8,128)} %all-reduce.2.cloned.1.call-done, s32[]{:T(128)S(6)} %select_n.18, f32[64,1024]{1,0:T(8,128)S(1)} %fusion.18), kind=kOutput, calls=%fused_computation.16 | convolution fusion | flops 3221749760 | bytes 19136516 | tf_op jit(solution)/shard_map/rkj,jkc->rkc/dot_general | solution.py:37
  598.8 11.8 %fusion.15 = f32[64,4,1024]{2,0,1:T(8,128)} fusion(f32[1024,4,1024]{2,0,1:T(8,128)S(1)} %copy-done.1, f32[64,4,1024]{2,0,1:T(8,128)S(1)} %convolution_bitcast_fusion.6, f32[64,4,1024]{2,0,1:T(8,128)S(1)} %copy-done.4), kind=kOutput, calls=%fused_computation.15 | convolution fusion | flops 3221749760 | bytes 19922944 | tf_op jit(solution)/shard_map/rkj,jkc->rkc/dot_general | solution.py:38
  610.6 0.0 all-gather.10.cloned.1.call-start
  610.7 124.7 %all-gather.8.cloned.1.call-done = f32[1024,4,1024]{2,0,1:T(8,128)} async-done(((f32[64,4,1024]{2,0,1:T(8,128)}), f32[1024,4,1024]{2,0,1:T(8,128)}) %all-gather.8.cloned.1.call-update) | async-done | bytes 16777232 | tf_op jit(solution)/shard_map/all_gather | solution.py:36
  735.4 15.0 %convolution_bitcast_fusion.4 = f32[64,4,1024]{2,0,1:T(8,128)S(1)} fusion(f32[1024,4,1024]{2,0,1:T(8,128)} %all-gather.8.cloned.1.call-done, f32[1024,4,1024]{2,0,1:T(8,128)} %all-reduce.2.cloned.1.call-done, s32[]{:T(128)S(6)} %select_n.18, f32[64,1024]{1,0:T(8,128)S(1)} %fusion.18), kind=kOutput, calls=%fused_computation.13 | convolution fusion | flops 3221749760 | bytes 19136516 | tf_op jit(solution)/shard_map/rkj,jkc->rkc/dot_general | solution.py:37
  750.4 11.8 %fusion.14 = f32[64,4,1024]{2,0,1:T(8,128)} fusion(f32[1024,4,1024]{2,0,1:T(8,128)S(1)} %copy-done.2, f32[64,4,1024]{2,0,1:T(8,128)S(1)} %convolution_bitcast_fusion.4, f32[64,4,1024]{2,0,1:T(8,128)S(1)} %copy-done.5), kind=kOutput, calls=%fused_computation.12 | convolution fusion | flops 3221749760 | bytes 19922944 | tf_op jit(solution)/shard_map/rkj,jkc->rkc/dot_general | solution.py:38
  762.2 0.0 all-gather.12.cloned.1.call-start
  762.3 124.7 %all-gather.10.cloned.1.call-done = f32[1024,4,1024]{2,0,1:T(8,128)} async-done(((f32[64,4,1024]{2,0,1:T(8,128)}), f32[1024,4,1024]{2,0,1:T(8,128)}) %all-gather.10.cloned.1.call-update) | async-done | bytes 16777232 | tf_op jit(solution)/shard_map/all_gather | solution.py:36
  887.0 15.0 %convolution_bitcast_fusion.2 = f32[64,4,1024]{2,0,1:T(8,128)S(1)} fusion(f32[1024,4,1024]{2,0,1:T(8,128)} %all-gather.10.cloned.1.call-done, f32[1024,4,1024]{2,0,1:T(8,128)} %all-reduce.2.cloned.1.call-done, s32[]{:T(128)S(6)} %select_n.18, f32[64,1024]{1,0:T(8,128)S(1)} %fusion.18), kind=kOutput, calls=%fused_computation.10 | convolution fusion | flops 3221749760 | bytes 19136516 | tf_op jit(solution)/shard_map/rkj,jkc->rkc/dot_general | solution.py:37
  902.0 11.6 %fusion.16 = bf16[64,4,1024]{2,0,1:T(8,128)(2,1)} fusion(f32[1024,4,1024]{2,0,1:T(8,128)S(1)} %copy-done, f32[64,4,1024]{2,0,1:T(8,128)S(1)} %convolution_bitcast_fusion.2, f32[64,4,1024]{2,0,1:T(8,128)S(1)} %copy-done.3), kind=kOutput, calls=%fused_computation.17 | convolution fusion | flops 3222011904 | bytes 19398656 | tf_op jit(solution)/shard_map/rkj,jkc->rkc/dot_general | solution.py:38
  913.7 13.2 %constant_dynamic-slice_fusion = bf16[1,4096,1792]{2,1,0:T(8,128)(2,1)} fusion(bf16[2,4096,1792]{2,1,0:T(8,128)(2,1)} %param.5, s32[]{:T(128)S(6)} %select_n.17), kind=kLoop, calls=%fused_computation.24 | loop fusion | bytes 29360132 | tf_op jit(solution)/shard_map/jit(dynamic_index_in_dim)/dynamic_slice | solution.py:16
  926.9 59.4 %all-gather.12.cloned.1.call-done = bf16[1024,4,1024]{2,0,1:T(8,128)(2,1)} async-done(((bf16[64,4,1024]{2,0,1:T(8,128)(2,1)}), bf16[1024,4,1024]{2,0,1:T(8,128)(2,1)}) %all-gather.12.cloned.1.call-update) | async-done | bytes 8388624 | tf_op jit(solution)/shard_map/all_gather | solution.py:45
  986.3 25.9 %fusion.19 = f32[4,1024,1792]{2,1,0:T(8,128)} fusion(bf16[1024,4,1024]{2,0,1:T(8,128)(2,1)} %all-gather.12.cloned.1.call-done, bf16[4,1024,1792]{2,1,0:T(8,128)(2,1)} %bitcast.50), kind=kOutput, calls=%fused_computation.27 | convolution fusion | flops 15032385536 | bytes 52428800 | tf_op jit(solution)/shard_map/rkc,kcf->krf/dot_general | solution.py:43
  (18 shorter events, 0.1 us)
Async XLA Ops:
  6.5 338.6 %all-reduce.2.cloned.1.call-start = ((), (), s32[]{:S(2)}) async-start(), calls=%async_computation | async-start | bytes 33554432 | tf_op jit(solution)/shard_map/psum | solution.py:24
  44.3 389.5 %all-gather.14.cloned.1.call-start = ((), (), s32[]{:S(2)}) async-start(), calls=%async_computation.5 | async-start | bytes 4456448 | tf_op jit(solution)/shard_map/all_gather | solution.py:36
  386.0 197.5 %all-gather.6.cloned.1.call-start = ((), (), s32[]{:S(2)}) async-start(), calls=%async_computation.1 | async-start | bytes 17825792 | tf_op jit(solution)/shard_map/all_gather | solution.py:36
  458.3 140.4 %copy-start.4 = (f32[64,4,1024]{2,0,1:T(8,128)S(1)}, f32[64,4,1024]{2,0,1:T(8,128)}, u32[]{:S(2)}) copy-start(f32[64,4,1024]{2,0,1:T(8,128)} %fusion.10) | copy-start | bytes 3145732
  458.4 277.0 %all-gather.8.cloned.1.call-start = ((), (), s32[]{:S(2)}) async-start(), calls=%async_computation.2 | async-start | bytes 17825792 | tf_op jit(solution)/shard_map/all_gather | solution.py:36
  583.5 15.3 %copy-start.1 = (f32[1024,4,1024]{2,0,1:T(8,128)S(1)}, f32[1024,4,1024]{2,0,1:T(8,128)}, u32[]{:S(2)}) copy-start(f32[1024,4,1024]{2,0,1:T(8,128)} %all-gather.6.cloned.1.call-done) | copy-start | bytes 50331652
  610.6 139.8 %copy-start.5 = (f32[64,4,1024]{2,0,1:T(8,128)S(1)}, f32[64,4,1024]{2,0,1:T(8,128)}, u32[]{:S(2)}) copy-start(f32[64,4,1024]{2,0,1:T(8,128)} %fusion.15) | copy-start | bytes 3145732
  610.6 276.4 %all-gather.10.cloned.1.call-start = ((), (), s32[]{:S(2)}) async-start(), calls=%async_computation.3 | async-start | bytes 17825792 | tf_op jit(solution)/shard_map/all_gather | solution.py:36
  735.4 15.0 %copy-start.2 = (f32[1024,4,1024]{2,0,1:T(8,128)S(1)}, f32[1024,4,1024]{2,0,1:T(8,128)}, u32[]{:S(2)}) copy-start(f32[1024,4,1024]{2,0,1:T(8,128)} %all-gather.8.cloned.1.call-done) | copy-start | bytes 50331652
  762.2 139.8 %copy-start.3 = (f32[64,4,1024]{2,0,1:T(8,128)S(1)}, f32[64,4,1024]{2,0,1:T(8,128)}, u32[]{:S(2)}) copy-start(f32[64,4,1024]{2,0,1:T(8,128)} %fusion.14) | copy-start | bytes 3145732
  762.2 224.1 %all-gather.12.cloned.1.call-start = ((), (), s32[]{:S(2)}) async-start(), calls=%async_computation.4 | async-start | bytes 8912896 | tf_op jit(solution)/shard_map/all_gather | solution.py:45
  887.0 15.0 %copy-start = (f32[1024,4,1024]{2,0,1:T(8,128)S(1)}, f32[1024,4,1024]{2,0,1:T(8,128)}, u32[]{:S(2)}) copy-start(f32[1024,4,1024]{2,0,1:T(8,128)} %all-gather.10.cloned.1.call-done) | copy-start | bytes 50331652
Sparse Core Ops, SparseCore 0:
  44.4 300.6 all-reduce.1
  386.1 47.5 all-gather.13
  458.5 124.9 all-gather.5
  610.7 124.6 all-gather.7
  762.3 124.6 all-gather.9
  913.8 72.4 all-gather.11
where the time goes:
time: 1020 us
  waiting for transfers between devices  782 us (77%)
  matrix products  148 us (15%)
  blocking collectives  37.3 us (4%)
  local copies, waits for them, and re-layouts  33.2 us (3%)
  between operations  15.4 us (2%)
    all_gather x4, waiting for transfers between devices, local(): whole = lax.all_gather(iterate, 'dp', axis=0, tiled=True)  422 us
    psum x1, waiting for transfers between devices, local(): lax.psum(jnp.einsum('tkr,tkc->rkc', blocks, blocks, preferred_element_typ...  301 us
    all_gather x1, waiting for transfers between devices, local(): lax.all_gather(inverse, 'dp', axis=0, tiled=True)  59.4 us
    dot_general x4, matrix products, local(): jnp.einsum('rkj,jkc->rkc', factor, whole, precision=lax.Precision.HIGHEST)  57 us
    dot_general x4, matrix products, local(): jnp.einsum('rkj,jkc->rkc', product, whole, precision=lax.Precision.HIGHEST)  48 us
    psum x1, blocking collectives, local(): block_squares = lax.psum(jnp.sum(factor * factor, axis=(0, 2)), 'dp')  31.8 us
    dot_general x1, matrix products, local(): jnp.einsum('rkc,kcf->krf', lax.all_gather(inverse, 'dp', axis=0, tiled=Tr...  25.9 us
  transfers between devices with their start and end apart: 6, of which 6 were waited for; matrix products, arithmetic and copies ran while one was open for 1% of the time, Pallas kernels for 0%

commit v1 on v0

--- a/solution.py
+++ b/solution.py
@@ -33,7 +33,14 @@
     largest = lax.pmax(jnp.max(block_squares), "tensor")
     iterate = jnp.broadcast_to(identity / jnp.sqrt(largest), factor.shape)
     for sweep in range(ITERS):
-        whole = lax.all_gather(iterate, "dp", axis=0, tiled=True)
+        ring = [iterate]
+        for hop in range(15):
+            ring.append(lax.ppermute(ring[-1], "dp", [(dev, (dev + 1) % 16) for dev in range(16)]))
+        whole = jnp.roll(
+            jnp.concatenate(ring[::-1], axis=0),
+            (lax.axis_index("dp") + 1) * ring[0].shape[0],
+            axis=0,
+        )
         product = jnp.einsum("rkj,jkc->rkc", factor, whole, precision=lax.Precision.HIGHEST)
         iterate = 2.0 * iterate - jnp.einsum(
             "rkj,jkc->rkc", product, whole, precision=lax.Precision.HIGHEST

time: 1020 us -> 1740 us (1.71)
  waiting for transfers between devices: 782 us -> 1370 us
  local copies, waits for them, and re-layouts: 33.2 us -> 123 us
  matrix products: 148 us -> 176 us
    ppermute x0 -> x60, waiting for transfers between devices: none -> 1020 us  [local(): lax.ppermute(ring[-1], 'dp', [(dev, (dev + 1) % 16) for dev in range(16)])]
    all_gather x4 -> x0, waiting for transfers between devices: 422 us -> none  [local(): whole = lax.all_gather(iterate, 'dp', axis=0, tiled=True)]
    unnamed x13 -> x93, local copies, waits for them, and re-layouts: 12 us -> 97.3 us
    dot_general x4, matrix products: 48 us -> 66.3 us  [local(): jnp.einsum('rkj,jkc->rkc', product, whole, precision=lax.Precision.HIGHEST)]
  transfers between devices with their start and end apart: 6 -> 62, of which waited for: 6 -> 62; matrix products, arithmetic and copies ran while one was open for 1% -> 1% of each run, Pallas kernels for 0% -> 0%
where the time goes in v1:
time: 1740 us; the launch traced here: 1730 us
  waiting for transfers between devices  1370 us (79%)
  matrix products  176 us (10%)
  local copies, waits for them, and re-layouts  123 us (7%)
  blocking collectives  37.3 us (2%)
    ppermute x60, waiting for transfers between devices, local(): lax.ppermute(ring[-1], 'dp', [(dev, (dev + 1) % 16) for dev in range(16)])  1020 us
    psum x1, waiting for transfers between devices, local(): lax.psum(jnp.einsum('tkr,tkc->rkc', blocks, blocks, preferred_element_typ...  300 us
    unnamed x93, local copies, waits for them, and re-layouts  97.3 us
    dot_general x4, matrix products, local(): jnp.einsum('rkj,jkc->rkc', factor, whole, precision=lax.Precision.HIGHEST)  67 us
    dot_general x4, matrix products, local(): jnp.einsum('rkj,jkc->rkc', product, whole, precision=lax.Precision.HIGHEST)  66.3 us
    all_gather x1, waiting for transfers between devices, local(): lax.all_gather(inverse, 'dp', axis=0, tiled=True)  58.4 us
  transfers between devices with their start and end apart: 62, of which 62 were waited for; matrix products, arithmetic and copies ran while one was open for 1% of the time, Pallas kernels for 0%

profile of v1, /device:TPU:0, one launch (start us, length us, event | category | flops | bytes accessed | tf_op | source)
XLA Modules:
  0.0 1730.1 jit_solution(13687268420460057141)
XLA Ops:
  27.1 17.2 convolution_bitcast_fusion
  44.6 300.5 %all-reduce.2.cloned.1.call-done = f32[1024,4,1024]{0,2,1:T(8,128)} async-done(((f32[1024,4,1024]{0,2,1:T(8,128)}), f32[1024,4,1024]{0,2,1:T(8,128)}) %all-reduce.2.cloned.1.call-update) | async-done | bytes 16777232 | tf_op jit(solution)/shard_map/psum | solution.py:24
  347.4 31.8 %psum.15 = f32[4]{0:T(128)S(1)} all-reduce(f32[4]{0:T(128)S(1)} %multiply_reduce_fusion), channel_id=1, replica_groups=mesh['dp'=16,'tensor'=2] {'dp'}, use_global_device_ids=true, to_apply=%region_2.3 | all-reduce | flops 4 | bytes 32 | tf_op jit(solution)/shard_map/psum | solution.py:32
  403.2 16.9 collective-permute-done.1
  420.1 16.9 collective-permute-done.2
  438.1 16.9 collective-permute-done.3
  491.8 16.9 collective-permute-done.6
  509.7 16.9 collective-permute-done.7
  527.7 16.9 collective-permute-done.8
  545.6 16.9 collective-permute-done.9
  617.2 17.0 collective-permute-done.13
  634.3 17.2 collective-permute-done.14
  678.5 17.0 fusion.41
  779.6 16.9 collective-permute-done.19
  796.5 16.9 collective-permute-done.20
  813.5 16.9 collective-permute-done.21
  830.4 16.9 collective-permute-done.22
  847.3 16.9 collective-permute-done.23
  864.2 16.9 collective-permute-done.24
  881.1 16.9 collective-permute-done.25
  898.1 16.9 collective-permute-done.26
  915.0 16.9 collective-permute-done.27
  931.9 16.9 collective-permute-done.28
  948.8 16.9 collective-permute-done.29
  1033.2 16.9 collective-permute-done.31
  1050.2 16.9 collective-permute-done.32
  1067.1 16.9 collective-permute-done.33
  1084.0 16.9 collective-permute-done.34
  1100.9 16.9 collective-permute-done.35
  1608.4 17.3 subtract_convert_fusion
  1639.0 58.4 %all-gather.2.cloned.1.call-done = bf16[1024,4,1024]{2,0,1:T(8,128)(2,1)} async-done(((bf16[64,4,1024]{2,0,1:T(8,128)(2,1)}), bf16[1024,4,1024]{2,0,1:T(8,128)(2,1)}) %all-gather.2.cloned.1.call-update) | async-done | bytes 8388624 | tf_op jit(solution)/shard_map/all_gather | solution.py:52
  1697.4 25.7 %fusion.71 = f32[4,1024,1792]{2,1,0:T(8,128)} fusion(bf16[1024,4,1024]{2,0,1:T(8,128)(2,1)} %all-gather.2.cloned.1.call-done, bf16[4,1024,1792]{2,1,0:T(8,128)(2,1)} %bitcast.42), kind=kOutput, calls=%fused_computation.122 | convolution fusion | flops 15032385536 | bytes 52428800 | tf_op jit(solution)/shard_map/rkc,kcf->krf/dot_general | solution.py:50
  (212 shorter events, 823.8 us)
Async XLA Ops:
  6.5 338.6 %all-reduce.2.cloned.1.call-start = ((), (), s32[]{:S(2)}) async-start(), calls=%async_computation | async-start | bytes 33554432 | tf_op jit(solution)/shard_map/psum | solution.py:24
  44.3 1653.2 %all-gather.2.cloned.1.call-start = ((), (), s32[]{:S(2)}) async-start(), calls=%async_computation.1 | async-start | bytes 8912896 | tf_op jit(solution)/shard_map/all_gather | solution.py:52
  386.3 17.0 collective-permute-start
  420.1 16.9 collective-permute-start.2
  438.1 16.9 collective-permute-start.3
  491.8 16.9 collective-permute-start.6
  509.7 16.9 collective-permute-start.7
  527.7 16.9 collective-permute-start.8
  617.2 17.0 collective-permute-start.13
  634.2 17.2 collective-permute-start.14
  711.9 17.0 collective-permute-start.15
  813.5 16.9 collective-permute-start.21
  830.4 16.9 collective-permute-start.22
  847.3 16.9 collective-permute-start.23
  864.2 16.9 collective-permute-start.24
  881.1 16.9 collective-permute-start.25
  898.1 16.9 collective-permute-start.26
  915.0 16.9 collective-permute-start.27
  931.9 16.9 collective-permute-start.28
  948.8 16.9 collective-permute-start.29
  1016.1 17.2 collective-permute-start.30
  1033.2 16.9 collective-permute-start.31
  1050.2 16.9 collective-permute-start.32
  1067.1 16.9 collective-permute-start.33
  1084.0 16.9 collective-permute-start.34
  1100.9 16.9 collective-permute-start.35
  1117.9 16.9 collective-permute-start.36
  1253.2 16.9 collective-permute-start.44
  1320.3 17.4 %collective-permute-start.45 = (f32[64,4,1024]{2,0,1:T(8,128)S(1)}, f32[64,4,1024]{2,0,1:T(8,128)S(1)}, u32[]{:S(2)}, u32[]{:S(2)}) collective-permute-start(f32[64,4,1024]{2,0,1:T(8,128)S(1)} %multiply_subtract_fusion), channel_id=1, source_target_pairs={{0,2},{2,4},{4,6},{6,8},{8,10},{10,12},{12,14},{14,16},{16,18},{18... | collective-permute-start | bytes 3145736 | tf_op jit(solution)/shard_map/ppermute | solution.py:38
  1337.7 16.9 collective-permute-start.46
  1354.6 16.9 collective-permute-start.47
  1371.6 16.9 collective-permute-start.48
  (46 other events, 707.8 us)
Sparse Core Ops, SparseCore 0:
  44.4 300.6 all-reduce.1
  1625.8 71.5 all-gather.1
